TPU v7x, 32 devices: a whole 2x2x4 slice. The times are simulated.
32 devices in a mesh: gx: 4 (over z), gy: 4 (over y, x), gz: 2 (over core).
Axes of the slice: x: 2, y: 2, z: 4, core: 2. Of those that a mesh axis runs over, the one named last changes fastest.
Arguments:
- signal: float32 [16, 131072], P(None, ('gx', 'gy', 'gz')), may hold values from -6 to 6
- order: int32 [131072], P(('gx', 'gy', 'gz')), may hold values from 0 to 4095, as said below
- near_tiles: bfloat16 [512, 3, 256, 256], P(('gx', 'gy', 'gz')), may hold values from -0.21875 to 0.21875
- near_list: int32 [512, 3], P(('gx', 'gy', 'gz')), may hold values from 0 to 511, as said below
- leaf_basis: bfloat16 [512, 64, 256], P(('gx', 'gy', 'gz')), may hold values from -0.375 to 0.375
- leaf_transfer: bfloat16 [512, 64, 64], P(('gx', 'gy', 'gz')), may hold values from -0.5 to 0.5
- leaf_coupling: bfloat16 [512, 64, 192], P(('gx', 'gy', 'gz')), may hold values from -0.4375 to 0.4375
- leaf_links: int32 [512, 3], P(('gx', 'gy', 'gz')), may hold values from 0 to 511, as said below
- device_transfer: bfloat16 [32, 64, 64], P(('gx', 'gy', 'gz')), may hold values from -0.5 to 0.5
- device_coupling: bfloat16 [32, 64, 192], P(('gx', 'gy', 'gz')), may hold values from -0.15625 to 0.15625
- device_links: int32 [32, 3], P(('gx', 'gy', 'gz')), may hold values from 0 to 31, as said below
- block_transfer: bfloat16 [16, 64, 64], P(('gx', 'gy')), may hold values from -0.5 to 0.5
- block_coupling: bfloat16 [16, 64, 192], P(('gx', 'gy')), may hold values from -0.15625 to 0.15625
- block_links: int32 [16, 3], P(('gx', 'gy')), may hold values from 0 to 15, as said below
- top_coupling: bfloat16 [4, 64, 192], P('gx'), may hold values from -0.109375 to 0.109375
- top_links: int32 [4, 3], P('gx'), may hold values from 0 to 3, as said below
Outputs:
- smoothed: float32 [16, 131072], P(None, ('gx', 'gy', 'gz'))
- twice: float32 [16, 131072], P(None, ('gx', 'gy', 'gz'))
Inputs may be any that keep to these rules, and one draw needn't show every extreme that they name: `order`: each device's block of 4096 consecutive entries is a permutation of 0 to 4095. `near_list`: row i holds i first, then two different leaves j with 1 <= |j - i| <= 2. `leaf_links`: row i holds three different leaves j with 2 <= |j - i| <= 4. `device_links`: row i holds three different device clusters j with 1 <= |j - i| <= 3. `block_links`: row i holds three different second-level clusters other than i. `top_links`: row i holds three different first-level clusters other than i.
All inputs are finite; a program needn't handle non-finite values.
Results may differ from a plain program's by a relative error of at most 0.0043.
Values may be sent and summed in bfloat16 or wider, within the bound.
No kernel may reach another device: no remote copies, remote signals or barrier semaphores. Data moves between devices by JAX's collectives and lax.ppermute only.
A program may use at most 64 MiB of HBM per device.

v0:
```python
import jax
import jax.numpy as jnp
from jax import lax
from jax.sharding import PartitionSpec as P

NEAR_REACH = 2
LINK_REACH = 4
DEVICE_REACH = 3
HIGH = lax.Precision.HIGHEST


def shifted(block, axis, distance):
    devices = range(lax.axis_size(axis))
    route = [(i - distance, i) for i in devices if i - distance in devices]
    return lax.ppermute(block, axis, route)


def couple(picked, coupling):
    rank_dim = coupling.shape[0]
    link_count = picked.shape[0]
    table = coupling.astype(jnp.float32).reshape(rank_dim, link_count, rank_dim)
    return jnp.einsum("jrk,kjm->rm", picked, table, precision=HIGH)


def spread_down(parent, transfer):
    return jnp.dot(parent, transfer.astype(jnp.float32).T, precision=HIGH)


def relay_side(own_moment, direction):
    window = own_moment[None][:0]
    for step in range(DEVICE_REACH):
        outgoing = jnp.concatenate([own_moment[None], window], axis=0)
        window = shifted(outgoing, ("gx", "gy", "gz"), direction)
    return window


def apply_matrix(
    leaves,
    near_tiles,
    near_list,
    leaf_basis,
    leaf_transfer,
    leaf_coupling,
    leaf_links,
    device_transfer,
    device_coupling,
    device_links,
    block_transfer,
    block_coupling,
    block_links,
    top_coupling,
    top_links,
):
    leaf_dev = leaves.shape[1]
    device = lax.axis_index(("gx", "gy", "gz"))
    first_leaf = device * leaf_dev
    rims = []
    for offset, edge in ((1, leaves[:, leaf_dev - NEAR_REACH :]), (-1, leaves[:, :NEAR_REACH])):
        rims.append(shifted(edge, ("gx", "gy", "gz"), offset))
    widened = jnp.concatenate([rims[0], leaves, rims[1]], axis=1)
    moments = jnp.einsum("rls,lks->rlk", leaves, leaf_basis, preferred_element_type=jnp.float32)
    edges = []
    for offset, edge in ((1, moments[:, leaf_dev - LINK_REACH :]), (-1, moments[:, :LINK_REACH])):
        edges.append(shifted(edge, ("gx", "gy", "gz"), offset))
    wide_moments = jnp.concatenate([edges[0], moments, edges[1]], axis=1)
    transfer_f = leaf_transfer.astype(jnp.float32)
    own_moment = jnp.einsum("rlk,lkm->rm", moments, transfer_f, precision=HIGH)
    block_term = jnp.dot(own_moment, device_transfer[0].astype(jnp.float32), precision=HIGH)
    block_moment = lax.psum(block_term, "gz")
    lower = relay_side(own_moment, 1)
    upper = relay_side(own_moment, -1)
    stacked = jnp.concatenate([lower[::-1], upper], axis=0)
    relative = device_links[0] - device
    position = relative + DEVICE_REACH - (relative > 0).astype(jnp.int32)
    device_picked = stacked[position]
    top_term = jnp.dot(block_moment, block_transfer[0].astype(jnp.float32), precision=HIGH)
    top_moment = lax.psum(top_term, "gy")
    every_top = lax.all_gather(top_moment[None], "gx", axis=0, tiled=True)
    every_block = lax.all_gather(block_moment[None], ("gx", "gy"), axis=0, tiled=True)
    top_field = couple(every_top[top_links[0]], top_coupling[0])
    block_field = couple(every_block[block_links[0]], block_coupling[0]) + spread_down(
        top_field, block_transfer[0]
    )
    device_field = couple(device_picked, device_coupling[0]) + spread_down(
        block_field, device_transfer[0]
    )
    local_links = leaf_links - first_leaf + LINK_REACH
    picked = wide_moments[:, local_links]
    rank_dim = leaf_coupling.shape[1]
    leaf_table = leaf_coupling.astype(jnp.float32).reshape(leaf_dev, rank_dim, -1, rank_dim)
    leaf_field = jnp.einsum("rljk,lkjm->rlm", picked, leaf_table, precision=HIGH)
    leaf_field = leaf_field + jnp.einsum("rm,lkm->rlk", device_field, transfer_f, precision=HIGH)
    far_part = jnp.einsum(
        "rlk,lks->rls",
        leaf_field.astype(jnp.bfloat16),
        leaf_basis,
        preferred_element_type=jnp.float32,
    )
    near_index = near_list - first_leaf + NEAR_REACH
    near_rows = widened[:, near_index]
    near_part = jnp.einsum(
        "rlns,lnst->rlt", near_rows, near_tiles, preferred_element_type=jnp.float32
    )
    return near_part + far_part


def shards(
    signal,
    order,
    near_tiles,
    near_list,
    leaf_basis,
    leaf_transfer,
    leaf_coupling,
    leaf_links,
    device_transfer,
    device_coupling,
    device_links,
    block_transfer,
    block_coupling,
    block_links,
    top_coupling,
    top_links,
):
    matrices = (
        near_tiles,
        near_list,
        leaf_basis,
        leaf_transfer,
        leaf_coupling,
        leaf_links,
        device_transfer,
        device_coupling,
        device_links,
        block_transfer,
        block_coupling,
        block_links,
        top_coupling,
        top_links,
    )
    rhs_count = signal.shape[0]
    leaf_count = near_tiles.shape[0]
    tree = jnp.take(signal, order, axis=1).astype(jnp.bfloat16).reshape(rhs_count, leaf_count, -1)
    first = apply_matrix(tree, *matrices)
    second = apply_matrix(first.astype(jnp.bfloat16), *matrices)
    empty = jnp.zeros_like(signal)
    smoothed = empty.at[:, order].set(first.reshape(rhs_count, -1))
    twice = empty.at[:, order].set(second.reshape(rhs_count, -1))
    return (smoothed, twice)


def solution(mesh):
    in_specs = (
        P(None, ("gx", "gy", "gz")),
        P(("gx", "gy", "gz")),
        P(("gx", "gy", "gz"), None, None, None),
        P(("gx", "gy", "gz"), None),
        P(("gx", "gy", "gz"), None, None),
        P(("gx", "gy", "gz"), None, None),
        P(("gx", "gy", "gz"), None, None),
        P(("gx", "gy", "gz"), None),
        P(("gx", "gy", "gz"), None, None),
        P(("gx", "gy", "gz"), None, None),
        P(("gx", "gy", "gz"), None),
        P(("gx", "gy"), None, None),
        P(("gx", "gy"), None, None),
        P(("gx", "gy"), None),
        P("gx", None, None),
        P("gx", None),
    )
    out_specs = (P(None, ("gx", "gy", "gz")), P(None, ("gx", "gy", "gz")))
    return jax.shard_map(shards, mesh=mesh, in_specs=in_specs, out_specs=out_specs, check_vma=False)
```

profile of v0, /device:TPU:4, one launch (start us, length us, event | category | flops | bytes accessed | tf_op | source)
XLA Modules:
  0.0 253.0 jit_solution(4829175544819906488)
XLA Ops:
  0.6 0.8 compare_and_fusion
  1.4 1.3 broadcast_clamp_fusion
  2.8 1.5 copy.38
  4.4 12.1 %gather_fusion = bf16[4096,16]{1,0:T(8,128)(2,1)S(1)} fusion(bf16[16,4096]{0,1:T(8,128)(2,1)S(1)} %copy.38, s32[4096]{0:T(1024)S(1)} %get-tuple-element.16), kind=kCustom, calls=%fused_computation | custom fusion | bytes 278528 | tf_op jit(solution)/shard_map/jit(_take)/gather | solution.py:143
  17.4 2.8 %collective-permute-start.7 = (f32[1,16,64]{2,1,0:T(8,128)S(1)}, f32[1,16,64]{2,1,0:T(8,128)S(1)}, u32[]{:S(2)}, u32[]{:S(2)}) collective-permute-start(f32[1,16,64]{2,1,0:T(8,128)S(1)} %bitcast.193), channel_id=1, source_target_pairs={{1,0},{2,1},{3,2},{4,3},{5,4},{6,5},{7,6},{8,7},{9,8},{10,9},{11,1... | collective-permute-start | bytes 12296 | tf_op jit(solution)/shard_map/ppermute | solution.py:15
  20.2 1.9 collective-permute-start.4
  22.2 2.6 %collective-permute-start = (bf16[16,2,256]{2,0,1:T(8,128)(2,1)S(1)}, bf16[16,2,256]{2,0,1:T(8,128)(2,1)S(1)}, u32[]{:S(2)}, u32[]{:S(2)}) collective-permute-start(bf16[16,2,256]{2,0,1:T(8,128)(2,1)S(1)} %get-tuple-element.14), channel_id=1, source_target_pairs={{0,1},{1,2},{2,3},{3,4},{4,5},{5,6},{6,7},{7,8},{8,9},{9,10},{10,1... | collective-permute-start | bytes 49160 | tf_op jit(solution)/shard_map/ppermute | solution.py:15
  24.8 3.8 %collective-permute-start.1 = (bf16[16,2,256]{2,0,1:T(8,128)(2,1)S(1)}, bf16[16,2,256]{2,0,1:T(8,128)(2,1)S(1)}, u32[]{:S(2)}, u32[]{:S(2)}) collective-permute-start(bf16[16,2,256]{2,0,1:T(8,128)(2,1)S(1)} %get-tuple-element.15), channel_id=1, source_target_pairs={{1,0},{2,1},{3,2},{4,3},{5,4},{6,5},{7,6},{8,7},{9,8},{10,9},{11,1... | collective-permute-start | bytes 49160 | tf_op jit(solution)/shard_map/ppermute | solution.py:15
  28.6 1.9 collective-permute-start.2
  31.3 3.6 %psum.28 = f32[16,64]{1,0:T(8,128)S(1)} all-reduce(f32[16,64]{1,0:T(8,128)S(1)} %fusion.23), channel_id=1, replica_groups=mesh['gx'=4,'gy'=4,'gz'=2] {'gz'}, use_global_device_ids=true, to_apply=%region_0.1 | all-reduce | flops 1024 | bytes 8192 | tf_op jit(solution)/shard_map/psum | solution.py:69
  34.9 35.5 %all-gather = f32[256,64]{1,0:T(8,128)S(1)} all-gather(f32[16,64]{1,0:T(8,128)S(1)} %psum.28), channel_id=2, replica_groups=mesh['gx'=4,'gy'=4,'gz'=2] {'gx','gy'}, dimensions={0}, use_global_device_ids=true | all-gather | bytes 69632 | tf_op jit(solution)/shard_map/all_gather | solution.py:79
  70.6 10.2 %psum.29 = f32[1,16,64]{2,1,0:T(8,128)S(1)} all-reduce(f32[1,16,64]{2,1,0:T(8,128)S(1)} %convolution_bitcast_fusion.11), channel_id=1, replica_groups=mesh['gx'=4,'gy'=4,'gz'=2] {'gy'}, use_global_device_ids=true, to_apply=%region_1.2 | all-reduce | flops 1024 | bytes 8192 | tf_op jit(solution)/shard_map/psum | solution.py:77
  80.8 13.1 %all_gather.13 = f32[4,16,64]{2,1,0:T(8,128)S(1)} all-gather(f32[1,16,64]{2,1,0:T(8,128)S(1)} %psum.29), channel_id=1, replica_groups=mesh['gx'=4,'gy'=4,'gz'=2] {'gx'}, dimensions={0}, use_global_device_ids=true | all-gather | bytes 20480 | tf_op jit(solution)/shard_map/all_gather | solution.py:78
  95.9 1.9 collective-permute-start.5
  97.8 4.5 %collective-permute-start.8 = (f32[2,16,64]{2,1,0:T(8,128)S(1)}, f32[2,16,64]{2,1,0:T(8,128)S(1)}, u32[]{:S(2)}, u32[]{:S(2)}) collective-permute-start(f32[2,16,64]{2,1,0:T(8,128)S(1)} %get-tuple-element.25), channel_id=1, source_target_pairs={{1,0},{2,1},{3,2},{4,3},{5,4},{6,5},{7,6},{8,7},{9,8},{10,9},{11,1... | collective-permute-start | bytes 24584 | tf_op jit(solution)/shard_map/ppermute | solution.py:15
  103.0 2.3 collective-permute-start.3
  105.3 2.0 collective-permute-start.6
  107.3 4.4 %collective-permute-start.9 = (f32[3,16,64]{2,1,0:T(8,128)S(1)}, f32[3,16,64]{2,1,0:T(8,128)S(1)}, u32[]{:S(2)}, u32[]{:S(2)}) collective-permute-start(f32[3,16,64]{2,1,0:T(8,128)S(1)} %get-tuple-element.23), channel_id=1, source_target_pairs={{1,0},{2,1},{3,2},{4,3},{5,4},{6,5},{7,6},{8,7},{9,8},{10,9},{11,1... | collective-permute-start | bytes 36872 | tf_op jit(solution)/shard_map/ppermute | solution.py:15
  112.4 3.7 %convolution_bitcast_fusion.1 = f32[16,16,256]{2,1,0:T(8,128)S(1)} fusion(bf16[16,16,3,256]{3,0,2,1:T(8,128)(2,1)S(1)} %bitcast.178, bf16[16,3,256,256]{3,2,1,0:T(8,128)(2,1)} %param.18), kind=kOutput, calls=%fused_computation.17 | convolution fusion | flops 100663296 | bytes 6946816 | tf_op jit(solution)/shard_map/rlns,lnst->rlt/dot_general | solution.py:101
  117.6 0.7 fusion.37
  118.3 0.9 fusion.3
  120.8 1.9 collective-permute-start.17
  122.7 2.4 collective-permute-start.14
  125.8 2.5 psum.30
  128.3 34.8 %all-gather.1 = f32[256,64]{1,0:T(8,128)S(1)} all-gather(f32[16,64]{1,0:T(8,128)S(1)} %psum.30), channel_id=3, replica_groups=mesh['gx'=4,'gy'=4,'gz'=2] {'gx','gy'}, dimensions={0}, use_global_device_ids=true | all-gather | bytes 69632 | tf_op jit(solution)/shard_map/all_gather | solution.py:79
  163.1 1.9 collective-permute-start.10
  165.0 4.5 %collective-permute-start.11 = (bf16[16,2,256]{2,0,1:T(8,128)(2,1)}, bf16[16,2,256]{2,0,1:T(8,128)(2,1)}, u32[]{:S(2)}, u32[]{:S(2)}) collective-permute-start(bf16[16,2,256]{2,0,1:T(8,128)(2,1)} %get-tuple-element.11), channel_id=1, source_target_pairs={{1,0},{2,1},{3,2},{4,3},{5,4},{6,5},{7,6},{8,7},{9,8},{10,9},{11,1... | collective-permute-start | bytes 49160 | tf_op jit(solution)/shard_map/ppermute | solution.py:15
  169.6 10.1 %psum.31 = f32[1,16,64]{2,1,0:T(8,128)S(1)} all-reduce(f32[1,16,64]{2,1,0:T(8,128)S(1)} %convolution_bitcast_fusion.7), channel_id=1, replica_groups=mesh['gx'=4,'gy'=4,'gz'=2] {'gy'}, use_global_device_ids=true, to_apply=%region_4.5 | all-reduce | flops 1024 | bytes 8192 | tf_op jit(solution)/shard_map/psum | solution.py:77
  179.7 13.1 %all_gather.15 = f32[4,16,64]{2,1,0:T(8,128)S(1)} all-gather(f32[1,16,64]{2,1,0:T(8,128)S(1)} %psum.31), channel_id=1, replica_groups=mesh['gx'=4,'gy'=4,'gz'=2] {'gx'}, dimensions={0}, use_global_device_ids=true | all-gather | bytes 20480 | tf_op jit(solution)/shard_map/all_gather | solution.py:78
  193.6 1.9 collective-permute-start.12
  197.0 1.9 collective-permute-start.15
  198.9 4.5 %collective-permute-start.18 = (f32[2,16,64]{2,1,0:T(8,128)}, f32[2,16,64]{2,1,0:T(8,128)}, u32[]{:S(2)}, u32[]{:S(2)}) collective-permute-start(f32[2,16,64]{2,1,0:T(8,128)} %get-tuple-element.21), channel_id=1, source_target_pairs={{1,0},{2,1},{3,2},{4,3},{5,4},{6,5},{7,6},{8,7},{9,8},{10,9},{11,1... | collective-permute-start | bytes 24584 | tf_op jit(solution)/shard_map/ppermute | solution.py:15
  203.5 0.8 fusion.17
  204.3 2.0 copy.51
  206.2 11.4 %scatter_custom_fusion = f32[16,4096]{0,1:T(8,128)S(1)} fusion(s32[4096]{0:T(1024)} %get-tuple-element.17, f32[4096,16]{1,0:T(8,128)} %copy.51, f32[]{:T(128)} %constant.15.clone.1), kind=kCustom, calls=%fused_computation.42 | custom fusion | bytes 262656 | tf_op jit(solution)/shard_map/scatter | solution.py:147
  217.7 1.3 copy.58
  218.9 2.4 collective-permute-start.13
  221.4 0.7 pad_maximum_fusion.9
  222.1 1.9 collective-permute-start.16
  224.0 4.7 %collective-permute-start.19 = (f32[3,16,64]{2,1,0:T(8,128)S(1)}, f32[3,16,64]{2,1,0:T(8,128)S(1)}, u32[]{:S(2)}, u32[]{:S(2)}) collective-permute-start(f32[3,16,64]{2,1,0:T(8,128)S(1)} %get-tuple-element.19), channel_id=1, source_target_pairs={{1,0},{2,1},{3,2},{4,3},{5,4},{6,5},{7,6},{8,7},{9,8},{10,9},{11,1... | collective-permute-start | bytes 36872 | tf_op jit(solution)/shard_map/ppermute | solution.py:15
  228.8 0.9 pad_maximum_fusion.3
  230.4 3.8 %convolution_bitcast_fusion = f32[16,16,256]{2,1,0:T(8,128)S(1)} fusion(bf16[16,16,3,256]{3,0,2,1:T(8,128)(2,1)S(1)} %bitcast.177, bf16[16,3,256,256]{3,2,1,0:T(8,128)(2,1)} %param.18), kind=kOutput, calls=%fused_computation.15 | convolution fusion | flops 100663296 | bytes 6946816 | tf_op jit(solution)/shard_map/rlns,lnst->rlt/dot_general | solution.py:101
  234.1 0.8 pad_maximum_fusion.1
  236.5 0.7 fusion.39
  237.2 0.9 fusion.4
  238.3 2.0 copy.57
  240.3 11.4 %scatter_custom_fusion.1 = f32[16,4096]{0,1:T(8,128)S(1)} fusion(s32[4096]{0:T(1024)} %get-tuple-element.17, f32[4096,16]{1,0:T(8,128)} %copy.57, f32[]{:T(128)} %constant.15.clone.1), kind=kCustom, calls=%fused_computation.40 | custom fusion | bytes 262656 | tf_op jit(solution)/shard_map/scatter | solution.py:148
  251.7 1.3 copy.59
  (136 shorter events, 12.8 us)
Async XLA Ops:
  0.6 16.3 %copy-start = (bf16[16,64,256]{2,1,0:T(8,128)(2,1)S(1)}, bf16[16,64,256]{2,1,0:T(8,128)(2,1)}, u32[]{:S(2)}) copy-start(bf16[16,64,256]{2,1,0:T(8,128)(2,1)} %param.20) | copy-start | bytes 1572868
  2.8 14.4 %copy-start.1 = (bf16[16,64,64]{2,1,0:T(8,128)(2,1)S(1)}, bf16[16,64,64]{2,1,0:T(8,128)(2,1)}, u32[]{:S(2)}) copy-start(bf16[16,64,64]{2,1,0:T(8,128)(2,1)} %param.21) | copy-start | bytes 393220
  4.2 26.3 %copy-start.23 = (s32[1,3]{1,0:T(1,128)S(1)}, s32[1,3]{1,0:T(1,128)}, u32[]{:S(2)}) copy-start(s32[1,3]{1,0:T(1,128)} %param.26) | copy-start | bytes 40
  4.3 26.3 %copy-start.24 = (s32[1,3]{1,0:T(1,128)S(1)}, s32[1,3]{1,0:T(1,128)}, u32[]{:S(2)}) copy-start(s32[1,3]{1,0:T(1,128)} %param.29) | copy-start | bytes 40
  4.3 26.4 %copy-start.25 = (s32[1,3]{1,0:T(1,128)S(1)}, s32[1,3]{1,0:T(1,128)}, u32[]{:S(2)}) copy-start(s32[1,3]{1,0:T(1,128)} %param.31) | copy-start | bytes 40
  4.3 26.4 %copy-start.21 = (s32[16,3]{0,1:T(4,128)S(1)}, s32[16,3]{0,1:T(4,128)}, u32[]{:S(2)}) copy-start(s32[16,3]{0,1:T(4,128)} %param.23) | copy-start | bytes 580
  4.3 26.4 %copy-start.22 = (s32[16,3]{0,1:T(4,128)S(1)}, s32[16,3]{0,1:T(4,128)}, u32[]{:S(2)}) copy-start(s32[16,3]{0,1:T(4,128)} %param.19) | copy-start | bytes 580
  4.3 26.6 %copy-start.16 = (bf16[1,64,192]{2,1,0:T(8,128)(2,1)S(1)}, bf16[1,64,192]{2,1,0:T(8,128)(2,1)}, u32[]{:S(2)}) copy-start(bf16[1,64,192]{2,1,0:T(8,128)(2,1)} %param.28) | copy-start | bytes 73732
  4.3 26.7 %copy-start.17 = (bf16[1,64,192]{2,1,0:T(8,128)(2,1)S(1)}, bf16[1,64,192]{2,1,0:T(8,128)(2,1)}, u32[]{:S(2)}) copy-start(bf16[1,64,192]{2,1,0:T(8,128)(2,1)} %param.30) | copy-start | bytes 73732
  4.3 26.8 %copy-start.8 = (bf16[1,64,64]{2,1,0:T(8,128)(2,1)S(1)}, bf16[1,64,64]{2,1,0:T(8,128)(2,1)}, u32[]{:S(2)}) copy-start(bf16[1,64,64]{2,1,0:T(8,128)(2,1)} %param.24) | copy-start | bytes 24580
  4.3 66.1 %copy-start.7 = (bf16[1,64,64]{2,1,0:T(8,128)(2,1)S(1)}, bf16[1,64,64]{2,1,0:T(8,128)(2,1)}, u32[]{:S(2)}) copy-start(bf16[1,64,64]{2,1,0:T(8,128)(2,1)} %param.27) | copy-start | bytes 24580
  16.5 85.9 %copy-start.18 = (bf16[1,64,192]{2,1,0:T(8,128)(2,1)S(1)}, bf16[1,64,192]{2,1,0:T(8,128)(2,1)}, u32[]{:S(2)}) copy-start(bf16[1,64,192]{2,1,0:T(8,128)(2,1)} %param.25) | copy-start | bytes 73732
  16.5 86.0 %copy-start.4 = (bf16[16,64,192]{2,1,0:T(8,128)(2,1)S(1)}, bf16[16,64,192]{2,1,0:T(8,128)(2,1)}, u32[]{:S(2)}) copy-start(bf16[16,64,192]{2,1,0:T(8,128)(2,1)} %param.22) | copy-start | bytes 1179652
  17.4 78.5 %collective-permute-start.7 = (f32[1,16,64]{2,1,0:T(8,128)S(1)}, f32[1,16,64]{2,1,0:T(8,128)S(1)}, u32[]{:S(2)}, u32[]{:S(2)}) collective-permute-start(f32[1,16,64]{2,1,0:T(8,128)S(1)} %bitcast.193), channel_id=1, source_target_pairs={{1,0},{2,1},{3,2},{4,3},{5,4},{6,5},{7,6},{8,7},{9,8},{10,9},{11,1... | collective-permute-start | bytes 12296 | tf_op jit(solution)/shard_map/ppermute | solution.py:15
  20.2 75.7 %collective-permute-start.4 = (f32[1,16,64]{2,1,0:T(8,128)S(1)}, f32[1,16,64]{2,1,0:T(8,128)S(1)}, u32[]{:S(2)}, u32[]{:S(2)}) collective-permute-start(f32[1,16,64]{2,1,0:T(8,128)S(1)} %bitcast.194), channel_id=1, source_target_pairs={{0,1},{1,2},{2,3},{3,4},{4,5},{5,6},{6,7},{7,8},{8,9},{9,10},{10,1... | collective-permute-start | bytes 12296 | tf_op jit(solution)/shard_map/ppermute | solution.py:15
  22.2 85.2 %collective-permute-start = (bf16[16,2,256]{2,0,1:T(8,128)(2,1)S(1)}, bf16[16,2,256]{2,0,1:T(8,128)(2,1)S(1)}, u32[]{:S(2)}, u32[]{:S(2)}) collective-permute-start(bf16[16,2,256]{2,0,1:T(8,128)(2,1)S(1)} %get-tuple-element.14), channel_id=1, source_target_pairs={{0,1},{1,2},{2,3},{3,4},{4,5},{5,6},{6,7},{7,8},{8,9},{9,10},{10,1... | collective-permute-start | bytes 49160 | tf_op jit(solution)/shard_map/ppermute | solution.py:15
  24.8 87.0 %collective-permute-start.1 = (bf16[16,2,256]{2,0,1:T(8,128)(2,1)S(1)}, bf16[16,2,256]{2,0,1:T(8,128)(2,1)S(1)}, u32[]{:S(2)}, u32[]{:S(2)}) collective-permute-start(bf16[16,2,256]{2,0,1:T(8,128)(2,1)S(1)} %get-tuple-element.15), channel_id=1, source_target_pairs={{1,0},{2,1},{3,2},{4,3},{5,4},{6,5},{7,6},{8,7},{9,8},{10,9},{11,1... | collective-permute-start | bytes 49160 | tf_op jit(solution)/shard_map/ppermute | solution.py:15
  28.6 87.5 %collective-permute-start.2 = (f32[16,4,64]{2,0,1:T(8,128)S(1)}, f32[16,4,64]{2,0,1:T(8,128)S(1)}, u32[]{:S(2)}, u32[]{:S(2)}) collective-permute-start(f32[16,4,64]{2,0,1:T(8,128)S(1)} %get-tuple-element.12), channel_id=1, source_target_pairs={{0,1},{1,2},{2,3},{3,4},{4,5},{5,6},{6,7},{7,8},{8,9},{9,10},{10,1... | collective-permute-start | bytes 49160 | tf_op jit(solution)/shard_map/ppermute | solution.py:15
  30.7 86.1 %copy-start.20 = (s32[1024]{0:T(1024)}, s32[1024]{0:T(1024)S(1)}, u32[]{:S(2)}) copy-start(s32[1024]{0:T(1024)S(1)} %pad_clamp_fusion.2) | copy-start | bytes 12292
  95.7 20.5 %copy-start.12 = (s32[1024]{0:T(1024)}, s32[1024]{0:T(1024)S(1)}, u32[]{:S(2)}) copy-start(s32[1024]{0:T(1024)S(1)} %pad_clamp_fusion.3) | copy-start | bytes 12292
  95.9 7.0 %collective-permute-start.5 = (f32[2,16,64]{2,1,0:T(8,128)S(1)}, f32[2,16,64]{2,1,0:T(8,128)S(1)}, u32[]{:S(2)}, u32[]{:S(2)}) collective-permute-start(f32[2,16,64]{2,1,0:T(8,128)S(1)} %get-tuple-element.24), channel_id=1, source_target_pairs={{0,1},{1,2},{2,3},{3,4},{4,5},{5,6},{6,7},{7,8},{8,9},{9,10},{10,1... | collective-permute-start | bytes 24584 | tf_op jit(solution)/shard_map/ppermute | solution.py:15
  97.8 7.4 %collective-permute-start.8 = (f32[2,16,64]{2,1,0:T(8,128)S(1)}, f32[2,16,64]{2,1,0:T(8,128)S(1)}, u32[]{:S(2)}, u32[]{:S(2)}) collective-permute-start(f32[2,16,64]{2,1,0:T(8,128)S(1)} %get-tuple-element.25), channel_id=1, source_target_pairs={{1,0},{2,1},{3,2},{4,3},{5,4},{6,5},{7,6},{8,7},{9,8},{10,9},{11,1... | collective-permute-start | bytes 24584 | tf_op jit(solution)/shard_map/ppermute | solution.py:15
  102.4 13.7 %copy-start.14 = (s32[1024]{0:T(1024)}, s32[1024]{0:T(1024)S(1)}, u32[]{:S(2)}) copy-start(s32[1024]{0:T(1024)S(1)} %pad_clamp_fusion.4) | copy-start | bytes 12292
  102.6 14.9 %copy-start.5 = (bf16[1,64,192]{1,2,0:T(8,128)(2,1)}, bf16[1,64,192]{1,2,0:T(8,128)(2,1)S(1)}, u32[]{:S(2)}) copy-start(bf16[1,64,192]{1,2,0:T(8,128)(2,1)S(1)} %copy.44) | copy-start | bytes 73732
  103.0 13.2 %collective-permute-start.3 = (f32[16,4,64]{2,0,1:T(8,128)S(1)}, f32[16,4,64]{2,0,1:T(8,128)S(1)}, u32[]{:S(2)}, u32[]{:S(2)}) collective-permute-start(f32[16,4,64]{2,0,1:T(8,128)S(1)} %get-tuple-element.13), channel_id=1, source_target_pairs={{1,0},{2,1},{3,2},{4,3},{5,4},{6,5},{7,6},{8,7},{9,8},{10,9},{11,1... | collective-permute-start | bytes 49160 | tf_op jit(solution)/shard_map/ppermute | solution.py:15
  105.3 11.5 %collective-permute-start.6 = (f32[3,16,64]{2,1,0:T(8,128)S(1)}, f32[3,16,64]{2,1,0:T(8,128)S(1)}, u32[]{:S(2)}, u32[]{:S(2)}) collective-permute-start(f32[3,16,64]{2,1,0:T(8,128)S(1)} %get-tuple-element.22), channel_id=1, source_target_pairs={{0,1},{1,2},{2,3},{3,4},{4,5},{5,6},{6,7},{7,8},{8,9},{9,10},{10,1... | collective-permute-start | bytes 36872 | tf_op jit(solution)/shard_map/ppermute | solution.py:15
  107.3 9.5 %collective-permute-start.9 = (f32[3,16,64]{2,1,0:T(8,128)S(1)}, f32[3,16,64]{2,1,0:T(8,128)S(1)}, u32[]{:S(2)}, u32[]{:S(2)}) collective-permute-start(f32[3,16,64]{2,1,0:T(8,128)S(1)} %get-tuple-element.23), channel_id=1, source_target_pairs={{1,0},{2,1},{3,2},{4,3},{5,4},{6,5},{7,6},{8,7},{9,8},{10,9},{11,1... | collective-permute-start | bytes 36872 | tf_op jit(solution)/shard_map/ppermute | solution.py:15
  117.6 3.0 %copy-start.9 = (bf16[1,64,64]{2,1,0:T(8,128)(2,1)S(1)}, bf16[1,64,64]{2,1,0:T(8,128)(2,1)}, u32[]{:S(2)}) copy-start(bf16[1,64,64]{2,1,0:T(8,128)(2,1)} %param.24) | copy-start | bytes 24580
  119.5 86.8 %copy-start.3 = (bf16[16,16,256]{2,0,1:T(8,128)(2,1)}, bf16[16,16,256]{2,0,1:T(8,128)(2,1)S(1)}, u32[]{:S(2)}) copy-start(bf16[16,16,256]{2,0,1:T(8,128)(2,1)S(1)} %get-tuple-element.26) | copy-start | bytes 393220
  120.6 83.6 %copy-start.10 = (f32[16,64,1]{1,0,2:T(8,128)}, f32[16,64,1]{1,0,2:T(8,128)S(1)}, u32[]{:S(2)}) copy-start(f32[16,64,1]{1,0,2:T(8,128)S(1)} %fusion.38) | copy-start | bytes 12292
  120.8 75.6 %collective-permute-start.17 = (f32[1,16,64]{2,1,0:T(8,128)S(1)}, f32[1,16,64]{2,1,0:T(8,128)S(1)}, u32[]{:S(2)}, u32[]{:S(2)}) collective-permute-start(f32[1,16,64]{2,1,0:T(8,128)S(1)} %bitcast.197), channel_id=1, source_target_pairs={{1,0},{2,1},{3,2},{4,3},{5,4},{6,5},{7,6},{8,7},{9,8},{10,9},{11,1... | collective-permute-start | bytes 12296 | tf_op jit(solution)/shard_map/ppermute | solution.py:15
  122.7 73.7 %collective-permute-start.14 = (f32[1,16,64]{2,1,0:T(8,128)S(1)}, f32[1,16,64]{2,1,0:T(8,128)S(1)}, u32[]{:S(2)}, u32[]{:S(2)}) collective-permute-start(f32[1,16,64]{2,1,0:T(8,128)S(1)} %bitcast.198), channel_id=1, source_target_pairs={{0,1},{1,2},{2,3},{3,4},{4,5},{5,6},{6,7},{7,8},{8,9},{9,10},{10,1... | collective-permute-start | bytes 12296 | tf_op jit(solution)/shard_map/ppermute | solution.py:15
  163.1 60.9 %collective-permute-start.10 = (bf16[16,2,256]{2,0,1:T(8,128)(2,1)}, bf16[16,2,256]{2,0,1:T(8,128)(2,1)}, u32[]{:S(2)}, u32[]{:S(2)}) collective-permute-start(bf16[16,2,256]{2,0,1:T(8,128)(2,1)} %get-tuple-element.10), channel_id=1, source_target_pairs={{0,1},{1,2},{2,3},{3,4},{4,5},{5,6},{6,7},{7,8},{8,9},{9,10},{10,1... | collective-permute-start | bytes 49160 | tf_op jit(solution)/shard_map/ppermute | solution.py:15
  165.0 63.8 %collective-permute-start.11 = (bf16[16,2,256]{2,0,1:T(8,128)(2,1)}, bf16[16,2,256]{2,0,1:T(8,128)(2,1)}, u32[]{:S(2)}, u32[]{:S(2)}) collective-permute-start(bf16[16,2,256]{2,0,1:T(8,128)(2,1)} %get-tuple-element.11), channel_id=1, source_target_pairs={{1,0},{2,1},{3,2},{4,3},{5,4},{6,5},{7,6},{8,7},{9,8},{10,9},{11,1... | collective-permute-start | bytes 49160 | tf_op jit(solution)/shard_map/ppermute | solution.py:15
  193.6 40.5 %collective-permute-start.12 = (f32[16,4,64]{2,0,1:T(8,128)}, f32[16,4,64]{2,0,1:T(8,128)}, u32[]{:S(2)}, u32[]{:S(2)}) collective-permute-start(f32[16,4,64]{2,0,1:T(8,128)} %get-tuple-element.8), channel_id=1, source_target_pairs={{0,1},{1,2},{2,3},{3,4},{4,5},{5,6},{6,7},{7,8},{8,9},{9,10},{10,1... | collective-permute-start | bytes 49160 | tf_op jit(solution)/shard_map/ppermute | solution.py:15
  197.0 21.9 %collective-permute-start.15 = (f32[2,16,64]{2,1,0:T(8,128)}, f32[2,16,64]{2,1,0:T(8,128)}, u32[]{:S(2)}, u32[]{:S(2)}) collective-permute-start(f32[2,16,64]{2,1,0:T(8,128)} %get-tuple-element.20), channel_id=1, source_target_pairs={{0,1},{1,2},{2,3},{3,4},{4,5},{5,6},{6,7},{7,8},{8,9},{9,10},{10,1... | collective-permute-start | bytes 24584 | tf_op jit(solution)/shard_map/ppermute | solution.py:15
  198.9 22.4 %collective-permute-start.18 = (f32[2,16,64]{2,1,0:T(8,128)}, f32[2,16,64]{2,1,0:T(8,128)}, u32[]{:S(2)}, u32[]{:S(2)}) collective-permute-start(f32[2,16,64]{2,1,0:T(8,128)} %get-tuple-element.21), channel_id=1, source_target_pairs={{1,0},{2,1},{3,2},{4,3},{5,4},{6,5},{7,6},{8,7},{9,8},{10,9},{11,1... | collective-permute-start | bytes 24584 | tf_op jit(solution)/shard_map/ppermute | solution.py:15
  206.2 15.1 %copy-start.11 = (f32[16,64,1]{1,0,2:T(8,128)S(1)}, f32[16,64,1]{1,0,2:T(8,128)}, u32[]{:S(2)}) copy-start(f32[16,64,1]{1,0,2:T(8,128)} %copy-done.10) | copy-start | bytes 12292
  206.2 23.5 %copy-start.15 = (s32[1024]{0:T(1024)S(1)}, s32[1024]{0:T(1024)}, u32[]{:S(2)}) copy-start(s32[1024]{0:T(1024)} %copy-done.14) | copy-start | bytes 12292
  218.9 15.2 %collective-permute-start.13 = (f32[16,4,64]{2,0,1:T(8,128)}, f32[16,4,64]{2,0,1:T(8,128)S(1)}, u32[]{:S(2)}, u32[]{:S(2)}) collective-permute-start(f32[16,4,64]{2,0,1:T(8,128)} %get-tuple-element.9), channel_id=1, source_target_pairs={{1,0},{2,1},{3,2},{4,3},{5,4},{6,5},{7,6},{8,7},{9,8},{10,9},{11,1... | collective-permute-start | bytes 49160 | tf_op jit(solution)/shard_map/ppermute | solution.py:15
  222.1 13.4 %collective-permute-start.16 = (f32[3,16,64]{2,1,0:T(8,128)S(1)}, f32[3,16,64]{2,1,0:T(8,128)S(1)}, u32[]{:S(2)}, u32[]{:S(2)}) collective-permute-start(f32[3,16,64]{2,1,0:T(8,128)S(1)} %get-tuple-element.18), channel_id=1, source_target_pairs={{0,1},{1,2},{2,3},{3,4},{4,5},{5,6},{6,7},{7,8},{8,9},{9,10},{10,1... | collective-permute-start | bytes 36872 | tf_op jit(solution)/shard_map/ppermute | solution.py:15
  224.0 11.5 %collective-permute-start.19 = (f32[3,16,64]{2,1,0:T(8,128)S(1)}, f32[3,16,64]{2,1,0:T(8,128)S(1)}, u32[]{:S(2)}, u32[]{:S(2)}) collective-permute-start(f32[3,16,64]{2,1,0:T(8,128)S(1)} %get-tuple-element.19), channel_id=1, source_target_pairs={{1,0},{2,1},{3,2},{4,3},{5,4},{6,5},{7,6},{8,7},{9,8},{10,9},{11,1... | collective-permute-start | bytes 36872 | tf_op jit(solution)/shard_map/ppermute | solution.py:15
  230.3 4.6 %copy-start.13 = (s32[1024]{0:T(1024)S(1)}, s32[1024]{0:T(1024)}, u32[]{:S(2)}) copy-start(s32[1024]{0:T(1024)} %copy-done.12) | copy-start | bytes 12292
  230.3 5.9 %copy-start.6 = (bf16[1,64,192]{1,2,0:T(8,128)(2,1)S(1)}, bf16[1,64,192]{1,2,0:T(8,128)(2,1)}, u32[]{:S(2)}) copy-start(bf16[1,64,192]{1,2,0:T(8,128)(2,1)} %copy-done.5) | copy-start | bytes 73732
  230.3 5.9 %copy-start.19 = (f32[16,64]{1,0:T(8,128)S(1)}, f32[16,64]{1,0:T(8,128)}, u32[]{:S(2)}) copy-start(f32[16,64]{1,0:T(8,128)} %fusion.17) | copy-start | bytes 12292
  230.4 6.1 %copy-start.2 = (bf16[16,64,64]{2,1,0:T(8,128)(2,1)S(1)}, bf16[16,64,64]{2,1,0:T(8,128)(2,1)}, u32[]{:S(2)}) copy-start(bf16[16,64,64]{2,1,0:T(8,128)(2,1)} %param.21) | copy-start | bytes 393220
where the time goes:
time: 254 us; the launch traced here: 253 us
  blocking collectives  123 us (48%)
  starting transfers between devices  56.5 us (22%)
  local copies, waits for them, and re-layouts  51.6 us (20%)
  matrix products  14.8 us (6%)
  other arithmetic  5.39 us (2%)
    all_gather x2, blocking collectives, apply_matrix(): lax.all_gather(block_moment[None], ('gx', 'gy'), axis=0, tiled=True)  70.3 us
    ppermute x20, starting transfers between devices, shifted(): return lax.ppermute(block, axis, route)  56.5 us
    all_gather x2, blocking collectives, apply_matrix(): every_top = lax.all_gather(top_moment[None], 'gx', axis=0, tiled=True)  26.3 us
    psum x2, blocking collectives, apply_matrix(): top_moment = lax.psum(top_term, 'gy')  20.4 us
    gather x2, local copies, waits for them, and re-layouts, shards(): jnp.take(signal, order, axis=1).astype(jnp.bfloat16)  12.4 us
    scatter x1, local copies, waits for them, and re-layouts, shards(): smoothed = empty.at[:, order].set(first.reshape(rhs_count, -1))  11.4 us
    scatter x1, local copies, waits for them, and re-layouts, shards(): twice = empty.at[:, order].set(second.reshape(rhs_count, -1))  11.4 us
    dot_general x2, matrix products, apply_matrix(): jnp.einsum('rlns,lnst->rlt', near_rows, near_tiles, preferred_element_typ...  7.46 us
  transfers between devices with their start and end apart: 20, of which 0 were waited for; matrix products, arithmetic and copies ran while one was open for 13% of the time, Pallas kernels for 0%

commit v1 on v0

--- a/solution.py
+++ b/solution.py
@@ -76,7 +76,12 @@
     top_term = jnp.dot(block_moment, block_transfer[0].astype(jnp.float32), precision=HIGH)
     top_moment = lax.psum(top_term, "gy")
     every_top = lax.all_gather(top_moment[None], "gx", axis=0, tiled=True)
-    every_block = lax.all_gather(block_moment[None], ("gx", "gy"), axis=0, tiled=True)
+    every_block = jnp.concatenate(
+        lax.all_to_all(
+            jnp.stack([block_moment[None]] * lax.axis_size(("gx", "gy"))), ("gx", "gy"), 0, 0
+        ),
+        axis=0,
+    )
     top_field = couple(every_top[top_links[0]], top_coupling[0])
     block_field = couple(every_block[block_links[0]], block_coupling[0]) + spread_down(
         top_field, block_transfer[0]

time: 254 us -> 211 us (0.83)
  blocking collectives: 123 us -> 51.8 us
  starting transfers between devices: 56.5 us -> 73.6 us
  local copies, waits for them, and re-layouts: 51.6 us -> 58.2 us
    all_gather x2 -> x0, blocking collectives: 70.3 us -> none  [apply_matrix(): lax.all_gather(block_moment[None], ('gx', 'gy'), axis=0, tiled=True)]
    all_to_all x0 -> x2, starting transfers between devices: none -> 15 us  [apply_matrix(): lax.all_to_all(jnp.stack([block_moment[None]] * lax.axis_size(('gx', 'gy'...]
    gather x2, local copies, waits for them, and re-layouts: 12.4 us -> 16.6 us  [shards(): jnp.take(signal, order, axis=1).astype(jnp.bfloat16)]
    unnamed x59 -> x65, local copies, waits for them, and re-layouts: 4.88 us -> 6.56 us
  transfers between devices with their start and end apart: 20 -> 22, of which waited for: 0 -> 0; matrix products, arithmetic and copies ran while one was open for 13% -> 17% of each run, Pallas kernels for 0% -> 0%
where the time goes in v1:
time: 211 us; the launch traced here: 208 us
  starting transfers between devices  73.6 us (35%)
  local copies, waits for them, and re-layouts  58.2 us (28%)
  blocking collectives  51.8 us (25%)
  matrix products  14.8 us (7%)
  other arithmetic  7.83 us (4%)
    ppermute x20, starting transfers between devices, shifted(): return lax.ppermute(block, axis, route)  58.6 us
    all_gather x2, blocking collectives, apply_matrix(): every_top = lax.all_gather(top_moment[None], 'gx', axis=0, tiled=True)  26.3 us
    psum x2, blocking collectives, apply_matrix(): top_moment = lax.psum(top_term, 'gy')  19.5 us
    gather x2, local copies, waits for them, and re-layouts, shards(): jnp.take(signal, order, axis=1).astype(jnp.bfloat16)  16.6 us
    all_to_all x2, starting transfers between devices, apply_matrix(): lax.all_to_all(jnp.stack([block_moment[None]] * lax.axis_size(('gx', 'gy'...  15 us
    scatter x1, local copies, waits for them, and re-layouts, shards(): smoothed = empty.at[:, order].set(first.reshape(rhs_count, -1))  11.4 us
    scatter x1, local copies, waits for them, and re-layouts, shards(): twice = empty.at[:, order].set(second.reshape(rhs_count, -1))  11.4 us
    dot_general x2, matrix products, apply_matrix(): jnp.einsum('rlns,lnst->rlt', near_rows, near_tiles, preferred_element_typ...  7.43 us
  transfers between devices with their start and end apart: 22, of which 0 were waited for; matrix products, arithmetic and copies ran while one was open for 17% of the time, Pallas kernels for 0%

profile of v1, /device:TPU:4, one launch (start us, length us, event | category | flops | bytes accessed | tf_op | source)
XLA Modules:
  0.0 208.1 jit_solution(11078284941871337612)
XLA Ops:
  0.6 0.8 compare_and_fusion
  1.4 1.3 broadcast_clamp_fusion
  2.8 1.5 copy.38
  4.3 15.0 %gather_fusion = bf16[4096,16]{1,0:T(8,128)(2,1)} fusion(bf16[16,4096]{0,1:T(8,128)(2,1)S(1)} %copy.38, s32[4096]{0:T(1024)S(1)} %get-tuple-element.16), kind=kCustom, calls=%fused_computation | custom fusion | bytes 278528 | tf_op jit(solution)/shard_map/jit(_take)/gather | solution.py:148
  19.3 1.6 copy.39
  21.5 2.8 %collective-permute-start.7 = (f32[1,16,64]{2,1,0:T(8,128)S(1)}, f32[1,16,64]{2,1,0:T(8,128)S(1)}, u32[]{:S(2)}, u32[]{:S(2)}) collective-permute-start(f32[1,16,64]{2,1,0:T(8,128)S(1)} %bitcast.193), channel_id=1, source_target_pairs={{1,0},{2,1},{3,2},{4,3},{5,4},{6,5},{7,6},{8,7},{9,8},{10,9},{11,1... | collective-permute-start | bytes 12296 | tf_op jit(solution)/shard_map/ppermute | solution.py:15
  24.3 1.9 collective-permute-start.4
  26.2 2.6 %collective-permute-start = (bf16[16,2,256]{2,0,1:T(8,128)(2,1)S(1)}, bf16[16,2,256]{2,0,1:T(8,128)(2,1)S(1)}, u32[]{:S(2)}, u32[]{:S(2)}) collective-permute-start(bf16[16,2,256]{2,0,1:T(8,128)(2,1)S(1)} %get-tuple-element.14), channel_id=1, source_target_pairs={{0,1},{1,2},{2,3},{3,4},{4,5},{5,6},{6,7},{7,8},{8,9},{9,10},{10,1... | collective-permute-start | bytes 49160 | tf_op jit(solution)/shard_map/ppermute | solution.py:15
  28.9 3.8 %collective-permute-start.1 = (bf16[16,2,256]{2,0,1:T(8,128)(2,1)S(1)}, bf16[16,2,256]{2,0,1:T(8,128)(2,1)S(1)}, u32[]{:S(2)}, u32[]{:S(2)}) collective-permute-start(bf16[16,2,256]{2,0,1:T(8,128)(2,1)S(1)} %get-tuple-element.15), channel_id=1, source_target_pairs={{1,0},{2,1},{3,2},{4,3},{5,4},{6,5},{7,6},{8,7},{9,8},{10,9},{11,1... | collective-permute-start | bytes 49160 | tf_op jit(solution)/shard_map/ppermute | solution.py:15
  32.7 1.9 collective-permute-start.2
  34.8 3.6 %psum.28 = f32[16,64]{1,0:T(8,128)S(1)} all-reduce(f32[16,64]{1,0:T(8,128)S(1)} %fusion.23), channel_id=1, replica_groups=mesh['gx'=4,'gy'=4,'gz'=2] {'gz'}, use_global_device_ids=true, to_apply=%region_0.1 | all-reduce | flops 1024 | bytes 8192 | tf_op jit(solution)/shard_map/psum | solution.py:69
  39.2 8.2 %all-to-all-start = ((f32[16,1,1024]{2,1,0:T(1,128)}), f32[16,1,1024]{2,1,0:T(1,128)S(1)}, u32[]{:S(2)}, u32[]{:S(2)}) async-start(f32[16,1,1024]{2,1,0:T(1,128)} %reshape.287), calls=%async_computation | async-start | bytes 131072 | tf_op jit(solution)/shard_map/all_to_all | solution.py:80
  48.0 9.1 %psum.29 = f32[1,16,64]{2,1,0:T(8,128)S(1)} all-reduce(f32[1,16,64]{2,1,0:T(8,128)S(1)} %convolution_bitcast_fusion.11), channel_id=1, replica_groups=mesh['gx'=4,'gy'=4,'gz'=2] {'gy'}, use_global_device_ids=true, to_apply=%region_1.2 | all-reduce | flops 1024 | bytes 8192 | tf_op jit(solution)/shard_map/psum | solution.py:77
  57.0 13.1 %all_gather.6 = f32[4,16,64]{2,1,0:T(8,128)S(1)} all-gather(f32[1,16,64]{2,1,0:T(8,128)S(1)} %psum.29), channel_id=1, replica_groups=mesh['gx'=4,'gy'=4,'gz'=2] {'gx'}, dimensions={0}, use_global_device_ids=true | all-gather | bytes 20480 | tf_op jit(solution)/shard_map/all_gather | solution.py:78
  71.1 1.9 collective-permute-start.5
  73.0 4.5 %collective-permute-start.8 = (f32[2,16,64]{2,1,0:T(8,128)S(1)}, f32[2,16,64]{2,1,0:T(8,128)S(1)}, u32[]{:S(2)}, u32[]{:S(2)}) collective-permute-start(f32[2,16,64]{2,1,0:T(8,128)S(1)} %get-tuple-element.25), channel_id=1, source_target_pairs={{1,0},{2,1},{3,2},{4,3},{5,4},{6,5},{7,6},{8,7},{9,8},{10,9},{11,1... | collective-permute-start | bytes 24584 | tf_op jit(solution)/shard_map/ppermute | solution.py:15
  78.3 1.9 collective-permute-start.3
  80.2 2.4 %collective-permute-start.6 = (f32[3,16,64]{2,1,0:T(8,128)S(1)}, f32[3,16,64]{2,1,0:T(8,128)S(1)}, u32[]{:S(2)}, u32[]{:S(2)}) collective-permute-start(f32[3,16,64]{2,1,0:T(8,128)S(1)} %get-tuple-element.22), channel_id=1, source_target_pairs={{0,1},{1,2},{2,3},{3,4},{4,5},{5,6},{6,7},{7,8},{8,9},{9,10},{10,1... | collective-permute-start | bytes 36872 | tf_op jit(solution)/shard_map/ppermute | solution.py:15
  82.7 4.1 %collective-permute-start.9 = (f32[3,16,64]{2,1,0:T(8,128)S(1)}, f32[3,16,64]{2,1,0:T(8,128)S(1)}, u32[]{:S(2)}, u32[]{:S(2)}) collective-permute-start(f32[3,16,64]{2,1,0:T(8,128)S(1)} %get-tuple-element.23), channel_id=1, source_target_pairs={{1,0},{2,1},{3,2},{4,3},{5,4},{6,5},{7,6},{8,7},{9,8},{10,9},{11,1... | collective-permute-start | bytes 36872 | tf_op jit(solution)/shard_map/ppermute | solution.py:15
  87.4 3.7 %convolution_bitcast_fusion.1 = f32[16,16,256]{2,1,0:T(8,128)S(1)} fusion(bf16[16,16,3,256]{3,0,2,1:T(8,128)(2,1)S(1)} %bitcast.178, bf16[16,3,256,256]{3,2,1,0:T(8,128)(2,1)} %param.18), kind=kOutput, calls=%fused_computation.17 | convolution fusion | flops 100663296 | bytes 6946816 | tf_op jit(solution)/shard_map/rlns,lnst->rlt/dot_general | solution.py:106
  92.9 0.8 reduce
  95.8 0.9 fusion.3
  98.2 1.9 collective-permute-start.17
  100.1 2.4 %collective-permute-start.14 = (f32[1,16,64]{2,1,0:T(8,128)S(1)}, f32[1,16,64]{2,1,0:T(8,128)S(1)}, u32[]{:S(2)}, u32[]{:S(2)}) collective-permute-start(f32[1,16,64]{2,1,0:T(8,128)S(1)} %bitcast.198), channel_id=1, source_target_pairs={{0,1},{1,2},{2,3},{3,4},{4,5},{5,6},{6,7},{7,8},{8,9},{9,10},{10,1... | collective-permute-start | bytes 12296 | tf_op jit(solution)/shard_map/ppermute | solution.py:15
  103.2 2.5 %collective-permute-start.10 = (bf16[16,2,256]{2,0,1:T(8,128)(2,1)}, bf16[16,2,256]{2,0,1:T(8,128)(2,1)}, u32[]{:S(2)}, u32[]{:S(2)}) collective-permute-start(bf16[16,2,256]{2,0,1:T(8,128)(2,1)} %get-tuple-element.10), channel_id=1, source_target_pairs={{0,1},{1,2},{2,3},{3,4},{4,5},{5,6},{6,7},{7,8},{8,9},{9,10},{10,1... | collective-permute-start | bytes 49160 | tf_op jit(solution)/shard_map/ppermute | solution.py:15
  105.7 4.0 %collective-permute-start.11 = (bf16[16,2,256]{2,0,1:T(8,128)(2,1)}, bf16[16,2,256]{2,0,1:T(8,128)(2,1)}, u32[]{:S(2)}, u32[]{:S(2)}) collective-permute-start(bf16[16,2,256]{2,0,1:T(8,128)(2,1)} %get-tuple-element.11), channel_id=1, source_target_pairs={{1,0},{2,1},{3,2},{4,3},{5,4},{6,5},{7,6},{8,7},{9,8},{10,9},{11,1... | collective-permute-start | bytes 49160 | tf_op jit(solution)/shard_map/ppermute | solution.py:15
  109.7 2.5 %psum.30 = f32[16,64]{1,0:T(8,128)S(1)} all-reduce(f32[16,64]{1,0:T(8,128)S(1)} %fusion.19), channel_id=1, replica_groups=mesh['gx'=4,'gy'=4,'gz'=2] {'gz'}, use_global_device_ids=true, to_apply=%region_3.4 | all-reduce | flops 1024 | bytes 8192 | tf_op jit(solution)/shard_map/psum | solution.py:69
  112.3 10.4 %psum.31 = f32[1,16,64]{2,1,0:T(8,128)S(1)} all-reduce(f32[1,16,64]{2,1,0:T(8,128)S(1)} %convolution_bitcast_fusion.7), channel_id=1, replica_groups=mesh['gx'=4,'gy'=4,'gz'=2] {'gy'}, use_global_device_ids=true, to_apply=%region_4.5 | all-reduce | flops 1024 | bytes 8192 | tf_op jit(solution)/shard_map/psum | solution.py:77
  122.7 13.2 %all_gather.7 = f32[4,16,64]{2,1,0:T(8,128)S(1)} all-gather(f32[1,16,64]{2,1,0:T(8,128)S(1)} %psum.31), channel_id=1, replica_groups=mesh['gx'=4,'gy'=4,'gz'=2] {'gx'}, dimensions={0}, use_global_device_ids=true | all-gather | bytes 20480 | tf_op jit(solution)/shard_map/all_gather | solution.py:78
  137.1 1.9 collective-permute-start.15
  139.0 4.5 %collective-permute-start.18 = (f32[2,16,64]{2,1,0:T(8,128)}, f32[2,16,64]{2,1,0:T(8,128)}, u32[]{:S(2)}, u32[]{:S(2)}) collective-permute-start(f32[2,16,64]{2,1,0:T(8,128)} %get-tuple-element.21), channel_id=1, source_target_pairs={{1,0},{2,1},{3,2},{4,3},{5,4},{6,5},{7,6},{8,7},{9,8},{10,9},{11,1... | collective-permute-start | bytes 24584 | tf_op jit(solution)/shard_map/ppermute | solution.py:15
  143.5 0.8 convolution_bitcast_fusion.6
  144.3 1.9 collective-permute-start.12
  147.0 6.8 %all-to-all-start.1 = ((f32[16,1,1024]{2,1,0:T(1,128)}), f32[16,1,1024]{2,1,0:T(1,128)}, u32[]{:S(2)}, u32[]{:S(2)}) async-start(f32[16,1,1024]{2,1,0:T(1,128)} %reshape.289), calls=%async_computation.1 | async-start | bytes 131072 | tf_op jit(solution)/shard_map/all_to_all | solution.py:80
  153.8 2.0 copy.51
  155.8 11.4 %scatter_custom_fusion = f32[16,4096]{0,1:T(8,128)S(1)} fusion(s32[4096]{0:T(1024)} %get-tuple-element.17, f32[4096,16]{1,0:T(8,128)} %copy.51, f32[]{:T(128)} %constant.15.clone.1), kind=kCustom, calls=%fused_computation.42 | custom fusion | bytes 262656 | tf_op jit(solution)/shard_map/scatter | solution.py:152
  167.2 1.3 copy.58
  168.5 4.9 %collective-permute-start.13 = (f32[16,4,64]{2,0,1:T(8,128)}, f32[16,4,64]{2,0,1:T(8,128)S(1)}, u32[]{:S(2)}, u32[]{:S(2)}) collective-permute-start(f32[16,4,64]{2,0,1:T(8,128)} %get-tuple-element.9), channel_id=1, source_target_pairs={{1,0},{2,1},{3,2},{4,3},{5,4},{6,5},{7,6},{8,7},{9,8},{10,9},{11,1... | collective-permute-start | bytes 49160 | tf_op jit(solution)/shard_map/ppermute | solution.py:15
  174.1 1.9 collective-permute-start.16
  176.1 4.7 %collective-permute-start.19 = (f32[3,16,64]{2,1,0:T(8,128)S(1)}, f32[3,16,64]{2,1,0:T(8,128)S(1)}, u32[]{:S(2)}, u32[]{:S(2)}) collective-permute-start(f32[3,16,64]{2,1,0:T(8,128)S(1)} %get-tuple-element.19), channel_id=1, source_target_pairs={{1,0},{2,1},{3,2},{4,3},{5,4},{6,5},{7,6},{8,7},{9,8},{10,9},{11,1... | collective-permute-start | bytes 36872 | tf_op jit(solution)/shard_map/ppermute | solution.py:15
  180.8 0.9 pad_maximum_fusion.3
  182.5 3.7 %convolution_bitcast_fusion = f32[16,16,256]{2,1,0:T(8,128)S(1)} fusion(bf16[16,16,3,256]{3,0,2,1:T(8,128)(2,1)S(1)} %bitcast.177, bf16[16,3,256,256]{3,2,1,0:T(8,128)(2,1)} %param.18), kind=kOutput, calls=%fused_computation.15 | convolution fusion | flops 100663296 | bytes 6946816 | tf_op jit(solution)/shard_map/rlns,lnst->rlt/dot_general | solution.py:106
  186.3 0.8 pad_maximum_fusion.1
  188.5 1.6 reduce.1
  192.2 0.9 fusion.4
  193.4 2.0 copy.57
  195.4 11.4 %scatter_custom_fusion.1 = f32[16,4096]{0,1:T(8,128)S(1)} fusion(s32[4096]{0:T(1024)} %get-tuple-element.17, f32[4096,16]{1,0:T(8,128)} %copy.57, f32[]{:T(128)} %constant.15.clone.1), kind=kCustom, calls=%fused_computation.40 | custom fusion | bytes 262656 | tf_op jit(solution)/shard_map/scatter | solution.py:153
  206.8 1.3 copy.59
  (149 shorter events, 17.2 us)
Async XLA Ops:
  0.6 20.3 %copy-start = (bf16[16,64,256]{2,1,0:T(8,128)(2,1)S(1)}, bf16[16,64,256]{2,1,0:T(8,128)(2,1)}, u32[]{:S(2)}) copy-start(bf16[16,64,256]{2,1,0:T(8,128)(2,1)} %param.20) | copy-start | bytes 1572868
  2.8 18.5 %copy-start.1 = (bf16[16,64,64]{2,1,0:T(8,128)(2,1)S(1)}, bf16[16,64,64]{2,1,0:T(8,128)(2,1)}, u32[]{:S(2)}) copy-start(bf16[16,64,64]{2,1,0:T(8,128)(2,1)} %param.21) | copy-start | bytes 393220
  4.2 30.4 %copy-start.10 = (bf16[1,64,64]{2,1,0:T(8,128)(2,1)S(1)}, bf16[1,64,64]{2,1,0:T(8,128)(2,1)}, u32[]{:S(2)}) copy-start(bf16[1,64,64]{2,1,0:T(8,128)(2,1)} %param.24) | copy-start | bytes 24580
  4.3 43.1 %copy-start.24 = (s32[1,3]{1,0:T(1,128)S(1)}, s32[1,3]{1,0:T(1,128)}, u32[]{:S(2)}) copy-start(s32[1,3]{1,0:T(1,128)} %param.26) | copy-start | bytes 40
  4.3 43.1 %copy-start.25 = (s32[1,3]{1,0:T(1,128)S(1)}, s32[1,3]{1,0:T(1,128)}, u32[]{:S(2)}) copy-start(s32[1,3]{1,0:T(1,128)} %param.29) | copy-start | bytes 40
  4.3 43.1 %copy-start.26 = (s32[1,3]{1,0:T(1,128)S(1)}, s32[1,3]{1,0:T(1,128)}, u32[]{:S(2)}) copy-start(s32[1,3]{1,0:T(1,128)} %param.31) | copy-start | bytes 40
  4.3 43.2 %copy-start.22 = (s32[16,3]{0,1:T(4,128)S(1)}, s32[16,3]{0,1:T(4,128)}, u32[]{:S(2)}) copy-start(s32[16,3]{0,1:T(4,128)} %param.23) | copy-start | bytes 580
  4.3 43.2 %copy-start.23 = (s32[16,3]{0,1:T(4,128)S(1)}, s32[16,3]{0,1:T(4,128)}, u32[]{:S(2)}) copy-start(s32[16,3]{0,1:T(4,128)} %param.19) | copy-start | bytes 580
  4.3 43.4 %copy-start.17 = (bf16[1,64,192]{2,1,0:T(8,128)(2,1)S(1)}, bf16[1,64,192]{2,1,0:T(8,128)(2,1)}, u32[]{:S(2)}) copy-start(bf16[1,64,192]{2,1,0:T(8,128)(2,1)} %param.30) | copy-start | bytes 73732
  4.3 43.5 %copy-start.9 = (bf16[1,64,64]{2,1,0:T(8,128)(2,1)S(1)}, bf16[1,64,64]{2,1,0:T(8,128)(2,1)}, u32[]{:S(2)}) copy-start(bf16[1,64,64]{2,1,0:T(8,128)(2,1)} %param.27) | copy-start | bytes 24580
  19.3 58.3 %copy-start.18 = (bf16[1,64,192]{2,1,0:T(8,128)(2,1)S(1)}, bf16[1,64,192]{2,1,0:T(8,128)(2,1)}, u32[]{:S(2)}) copy-start(bf16[1,64,192]{2,1,0:T(8,128)(2,1)} %param.25) | copy-start | bytes 73732
  19.3 58.4 %copy-start.19 = (bf16[1,64,192]{2,1,0:T(8,128)(2,1)S(1)}, bf16[1,64,192]{2,1,0:T(8,128)(2,1)}, u32[]{:S(2)}) copy-start(bf16[1,64,192]{2,1,0:T(8,128)(2,1)} %param.28) | copy-start | bytes 73732
  19.3 58.5 %copy-start.4 = (bf16[16,64,192]{2,1,0:T(8,128)(2,1)S(1)}, bf16[16,64,192]{2,1,0:T(8,128)(2,1)}, u32[]{:S(2)}) copy-start(bf16[16,64,192]{2,1,0:T(8,128)(2,1)} %param.22) | copy-start | bytes 1179652
  21.5 49.6 %collective-permute-start.7 = (f32[1,16,64]{2,1,0:T(8,128)S(1)}, f32[1,16,64]{2,1,0:T(8,128)S(1)}, u32[]{:S(2)}, u32[]{:S(2)}) collective-permute-start(f32[1,16,64]{2,1,0:T(8,128)S(1)} %bitcast.193), channel_id=1, source_target_pairs={{1,0},{2,1},{3,2},{4,3},{5,4},{6,5},{7,6},{8,7},{9,8},{10,9},{11,1... | collective-permute-start | bytes 12296 | tf_op jit(solution)/shard_map/ppermute | solution.py:15
  24.3 46.8 %collective-permute-start.4 = (f32[1,16,64]{2,1,0:T(8,128)S(1)}, f32[1,16,64]{2,1,0:T(8,128)S(1)}, u32[]{:S(2)}, u32[]{:S(2)}) collective-permute-start(f32[1,16,64]{2,1,0:T(8,128)S(1)} %bitcast.194), channel_id=1, source_target_pairs={{0,1},{1,2},{2,3},{3,4},{4,5},{5,6},{6,7},{7,8},{8,9},{9,10},{10,1... | collective-permute-start | bytes 12296 | tf_op jit(solution)/shard_map/ppermute | solution.py:15
  26.2 56.4 %collective-permute-start = (bf16[16,2,256]{2,0,1:T(8,128)(2,1)S(1)}, bf16[16,2,256]{2,0,1:T(8,128)(2,1)S(1)}, u32[]{:S(2)}, u32[]{:S(2)}) collective-permute-start(bf16[16,2,256]{2,0,1:T(8,128)(2,1)S(1)} %get-tuple-element.14), channel_id=1, source_target_pairs={{0,1},{1,2},{2,3},{3,4},{4,5},{5,6},{6,7},{7,8},{8,9},{9,10},{10,1... | collective-permute-start | bytes 49160 | tf_op jit(solution)/shard_map/ppermute | solution.py:15
  28.9 57.8 %collective-permute-start.1 = (bf16[16,2,256]{2,0,1:T(8,128)(2,1)S(1)}, bf16[16,2,256]{2,0,1:T(8,128)(2,1)S(1)}, u32[]{:S(2)}, u32[]{:S(2)}) collective-permute-start(bf16[16,2,256]{2,0,1:T(8,128)(2,1)S(1)} %get-tuple-element.15), channel_id=1, source_target_pairs={{1,0},{2,1},{3,2},{4,3},{5,4},{6,5},{7,6},{8,7},{9,8},{10,9},{11,1... | collective-permute-start | bytes 49160 | tf_op jit(solution)/shard_map/ppermute | solution.py:15
  32.7 58.3 %collective-permute-start.2 = (f32[16,4,64]{2,0,1:T(8,128)S(1)}, f32[16,4,64]{2,0,1:T(8,128)S(1)}, u32[]{:S(2)}, u32[]{:S(2)}) collective-permute-start(f32[16,4,64]{2,0,1:T(8,128)S(1)} %get-tuple-element.12), channel_id=1, source_target_pairs={{0,1},{1,2},{2,3},{3,4},{4,5},{5,6},{6,7},{7,8},{8,9},{9,10},{10,1... | collective-permute-start | bytes 49160 | tf_op jit(solution)/shard_map/ppermute | solution.py:15
  39.2 53.2 %all-to-all-start = ((f32[16,1,1024]{2,1,0:T(1,128)}), f32[16,1,1024]{2,1,0:T(1,128)S(1)}, u32[]{:S(2)}, u32[]{:S(2)}) async-start(f32[16,1,1024]{2,1,0:T(1,128)} %reshape.287), calls=%async_computation | async-start | bytes 131072 | tf_op jit(solution)/shard_map/all_to_all | solution.py:80
  47.5 46.4 %copy-start.20 = (s32[1024]{0:T(1024)}, s32[1024]{0:T(1024)S(1)}, u32[]{:S(2)}) copy-start(s32[1024]{0:T(1024)S(1)} %pad_clamp_fusion.1) | copy-start | bytes 12292
  47.5 44.3 %copy-start.21 = (s32[1024]{0:T(1024)}, s32[1024]{0:T(1024)S(1)}, u32[]{:S(2)}) copy-start(s32[1024]{0:T(1024)S(1)} %pad_clamp_fusion.2) | copy-start | bytes 12292
  70.9 20.2 %copy-start.13 = (s32[1024]{0:T(1024)}, s32[1024]{0:T(1024)S(1)}, u32[]{:S(2)}) copy-start(s32[1024]{0:T(1024)S(1)} %pad_clamp_fusion.3) | copy-start | bytes 12292
  71.1 7.2 %collective-permute-start.5 = (f32[2,16,64]{2,1,0:T(8,128)S(1)}, f32[2,16,64]{2,1,0:T(8,128)S(1)}, u32[]{:S(2)}, u32[]{:S(2)}) collective-permute-start(f32[2,16,64]{2,1,0:T(8,128)S(1)} %get-tuple-element.24), channel_id=1, source_target_pairs={{0,1},{1,2},{2,3},{3,4},{4,5},{5,6},{6,7},{7,8},{8,9},{9,10},{10,1... | collective-permute-start | bytes 24584 | tf_op jit(solution)/shard_map/ppermute | solution.py:15
  73.0 7.2 %collective-permute-start.8 = (f32[2,16,64]{2,1,0:T(8,128)S(1)}, f32[2,16,64]{2,1,0:T(8,128)S(1)}, u32[]{:S(2)}, u32[]{:S(2)}) collective-permute-start(f32[2,16,64]{2,1,0:T(8,128)S(1)} %get-tuple-element.25), channel_id=1, source_target_pairs={{1,0},{2,1},{3,2},{4,3},{5,4},{6,5},{7,6},{8,7},{9,8},{10,9},{11,1... | collective-permute-start | bytes 24584 | tf_op jit(solution)/shard_map/ppermute | solution.py:15
  77.6 13.5 %copy-start.15 = (s32[1024]{0:T(1024)}, s32[1024]{0:T(1024)S(1)}, u32[]{:S(2)}) copy-start(s32[1024]{0:T(1024)S(1)} %pad_clamp_fusion.4) | copy-start | bytes 12292
  77.7 17.1 %copy-start.7 = (bf16[1,64,192]{1,2,0:T(8,128)(2,1)}, bf16[1,64,192]{1,2,0:T(8,128)(2,1)S(1)}, u32[]{:S(2)}) copy-start(bf16[1,64,192]{1,2,0:T(8,128)(2,1)S(1)} %copy.44) | copy-start | bytes 73732
  77.9 16.5 %copy-start.5 = (bf16[1,64,192]{1,2,0:T(8,128)(2,1)}, bf16[1,64,192]{1,2,0:T(8,128)(2,1)S(1)}, u32[]{:S(2)}) copy-start(bf16[1,64,192]{1,2,0:T(8,128)(2,1)S(1)} %copy.46) | copy-start | bytes 73732
  78.3 12.8 %collective-permute-start.3 = (f32[16,4,64]{2,0,1:T(8,128)S(1)}, f32[16,4,64]{2,0,1:T(8,128)S(1)}, u32[]{:S(2)}, u32[]{:S(2)}) collective-permute-start(f32[16,4,64]{2,0,1:T(8,128)S(1)} %get-tuple-element.13), channel_id=1, source_target_pairs={{1,0},{2,1},{3,2},{4,3},{5,4},{6,5},{7,6},{8,7},{9,8},{10,9},{11,1... | collective-permute-start | bytes 49160 | tf_op jit(solution)/shard_map/ppermute | solution.py:15
  80.2 11.5 %collective-permute-start.6 = (f32[3,16,64]{2,1,0:T(8,128)S(1)}, f32[3,16,64]{2,1,0:T(8,128)S(1)}, u32[]{:S(2)}, u32[]{:S(2)}) collective-permute-start(f32[3,16,64]{2,1,0:T(8,128)S(1)} %get-tuple-element.22), channel_id=1, source_target_pairs={{0,1},{1,2},{2,3},{3,4},{4,5},{5,6},{6,7},{7,8},{8,9},{9,10},{10,1... | collective-permute-start | bytes 36872 | tf_op jit(solution)/shard_map/ppermute | solution.py:15
  82.7 9.1 %collective-permute-start.9 = (f32[3,16,64]{2,1,0:T(8,128)S(1)}, f32[3,16,64]{2,1,0:T(8,128)S(1)}, u32[]{:S(2)}, u32[]{:S(2)}) collective-permute-start(f32[3,16,64]{2,1,0:T(8,128)S(1)} %get-tuple-element.23), channel_id=1, source_target_pairs={{1,0},{2,1},{3,2},{4,3},{5,4},{6,5},{7,6},{8,7},{9,8},{10,9},{11,1... | collective-permute-start | bytes 36872 | tf_op jit(solution)/shard_map/ppermute | solution.py:15
  96.9 58.9 %copy-start.3 = (bf16[16,16,256]{2,0,1:T(8,128)(2,1)}, bf16[16,16,256]{2,0,1:T(8,128)(2,1)S(1)}, u32[]{:S(2)}) copy-start(bf16[16,16,256]{2,0,1:T(8,128)(2,1)S(1)} %get-tuple-element.26) | copy-start | bytes 393220
  98.1 57.7 %copy-start.12 = (f32[16,64,1]{1,0,2:T(8,128)}, f32[16,64,1]{1,0,2:T(8,128)S(1)}, u32[]{:S(2)}) copy-start(f32[16,64,1]{1,0,2:T(8,128)S(1)} %fusion.38) | copy-start | bytes 12292
  98.2 38.2 %collective-permute-start.17 = (f32[1,16,64]{2,1,0:T(8,128)S(1)}, f32[1,16,64]{2,1,0:T(8,128)S(1)}, u32[]{:S(2)}, u32[]{:S(2)}) collective-permute-start(f32[1,16,64]{2,1,0:T(8,128)S(1)} %bitcast.197), channel_id=1, source_target_pairs={{1,0},{2,1},{3,2},{4,3},{5,4},{6,5},{7,6},{8,7},{9,8},{10,9},{11,1... | collective-permute-start | bytes 12296 | tf_op jit(solution)/shard_map/ppermute | solution.py:15
  100.1 36.3 %collective-permute-start.14 = (f32[1,16,64]{2,1,0:T(8,128)S(1)}, f32[1,16,64]{2,1,0:T(8,128)S(1)}, u32[]{:S(2)}, u32[]{:S(2)}) collective-permute-start(f32[1,16,64]{2,1,0:T(8,128)S(1)} %bitcast.198), channel_id=1, source_target_pairs={{0,1},{1,2},{2,3},{3,4},{4,5},{5,6},{6,7},{7,8},{8,9},{9,10},{10,1... | collective-permute-start | bytes 12296 | tf_op jit(solution)/shard_map/ppermute | solution.py:15
  103.2 72.8 %collective-permute-start.10 = (bf16[16,2,256]{2,0,1:T(8,128)(2,1)}, bf16[16,2,256]{2,0,1:T(8,128)(2,1)}, u32[]{:S(2)}, u32[]{:S(2)}) collective-permute-start(bf16[16,2,256]{2,0,1:T(8,128)(2,1)} %get-tuple-element.10), channel_id=1, source_target_pairs={{0,1},{1,2},{2,3},{3,4},{4,5},{5,6},{6,7},{7,8},{8,9},{9,10},{10,1... | collective-permute-start | bytes 49160 | tf_op jit(solution)/shard_map/ppermute | solution.py:15
  105.7 75.1 %collective-permute-start.11 = (bf16[16,2,256]{2,0,1:T(8,128)(2,1)}, bf16[16,2,256]{2,0,1:T(8,128)(2,1)}, u32[]{:S(2)}, u32[]{:S(2)}) collective-permute-start(bf16[16,2,256]{2,0,1:T(8,128)(2,1)} %get-tuple-element.11), channel_id=1, source_target_pairs={{1,0},{2,1},{3,2},{4,3},{5,4},{6,5},{7,6},{8,7},{9,8},{10,9},{11,1... | collective-permute-start | bytes 49160 | tf_op jit(solution)/shard_map/ppermute | solution.py:15
  137.1 31.4 %collective-permute-start.15 = (f32[2,16,64]{2,1,0:T(8,128)}, f32[2,16,64]{2,1,0:T(8,128)}, u32[]{:S(2)}, u32[]{:S(2)}) collective-permute-start(f32[2,16,64]{2,1,0:T(8,128)} %get-tuple-element.20), channel_id=1, source_target_pairs={{0,1},{1,2},{2,3},{3,4},{4,5},{5,6},{6,7},{7,8},{8,9},{9,10},{10,1... | collective-permute-start | bytes 24584 | tf_op jit(solution)/shard_map/ppermute | solution.py:15
  139.0 34.4 %collective-permute-start.18 = (f32[2,16,64]{2,1,0:T(8,128)}, f32[2,16,64]{2,1,0:T(8,128)}, u32[]{:S(2)}, u32[]{:S(2)}) collective-permute-start(f32[2,16,64]{2,1,0:T(8,128)} %get-tuple-element.21), channel_id=1, source_target_pairs={{1,0},{2,1},{3,2},{4,3},{5,4},{6,5},{7,6},{8,7},{9,8},{10,9},{11,1... | collective-permute-start | bytes 24584 | tf_op jit(solution)/shard_map/ppermute | solution.py:15
  144.3 41.9 %collective-permute-start.12 = (f32[16,4,64]{2,0,1:T(8,128)}, f32[16,4,64]{2,0,1:T(8,128)}, u32[]{:S(2)}, u32[]{:S(2)}) collective-permute-start(f32[16,4,64]{2,0,1:T(8,128)} %get-tuple-element.8), channel_id=1, source_target_pairs={{0,1},{1,2},{2,3},{3,4},{4,5},{5,6},{6,7},{7,8},{8,9},{9,10},{10,1... | collective-permute-start | bytes 49160 | tf_op jit(solution)/shard_map/ppermute | solution.py:15
  147.0 41.5 %all-to-all-start.1 = ((f32[16,1,1024]{2,1,0:T(1,128)}), f32[16,1,1024]{2,1,0:T(1,128)}, u32[]{:S(2)}, u32[]{:S(2)}) async-start(f32[16,1,1024]{2,1,0:T(1,128)} %reshape.289), calls=%async_computation.1 | async-start | bytes 131072 | tf_op jit(solution)/shard_map/all_to_all | solution.py:80
  168.5 17.8 %collective-permute-start.13 = (f32[16,4,64]{2,0,1:T(8,128)}, f32[16,4,64]{2,0,1:T(8,128)S(1)}, u32[]{:S(2)}, u32[]{:S(2)}) collective-permute-start(f32[16,4,64]{2,0,1:T(8,128)} %get-tuple-element.9), channel_id=1, source_target_pairs={{1,0},{2,1},{3,2},{4,3},{5,4},{6,5},{7,6},{8,7},{9,8},{10,9},{11,1... | collective-permute-start | bytes 49160 | tf_op jit(solution)/shard_map/ppermute | solution.py:15
  174.1 13.6 %collective-permute-start.16 = (f32[3,16,64]{2,1,0:T(8,128)S(1)}, f32[3,16,64]{2,1,0:T(8,128)S(1)}, u32[]{:S(2)}, u32[]{:S(2)}) collective-permute-start(f32[3,16,64]{2,1,0:T(8,128)S(1)} %get-tuple-element.18), channel_id=1, source_target_pairs={{0,1},{1,2},{2,3},{3,4},{4,5},{5,6},{6,7},{7,8},{8,9},{9,10},{10,1... | collective-permute-start | bytes 36872 | tf_op jit(solution)/shard_map/ppermute | solution.py:15
  176.1 11.7 %collective-permute-start.19 = (f32[3,16,64]{2,1,0:T(8,128)S(1)}, f32[3,16,64]{2,1,0:T(8,128)S(1)}, u32[]{:S(2)}, u32[]{:S(2)}) collective-permute-start(f32[3,16,64]{2,1,0:T(8,128)S(1)} %get-tuple-element.19), channel_id=1, source_target_pairs={{1,0},{2,1},{3,2},{4,3},{5,4},{6,5},{7,6},{8,7},{9,8},{10,9},{11,1... | collective-permute-start | bytes 36872 | tf_op jit(solution)/shard_map/ppermute | solution.py:15
  182.5 8.4 %copy-start.6 = (bf16[1,64,192]{1,2,0:T(8,128)(2,1)S(1)}, bf16[1,64,192]{1,2,0:T(8,128)(2,1)}, u32[]{:S(2)}) copy-start(bf16[1,64,192]{1,2,0:T(8,128)(2,1)} %copy-done.5) | copy-start | bytes 73732
  186.2 4.8 %copy-start.16 = (f32[16,64]{1,0:T(8,128)S(1)}, f32[16,64]{1,0:T(8,128)}, u32[]{:S(2)}) copy-start(f32[16,64]{1,0:T(8,128)} %convolution_bitcast_fusion.6) | copy-start | bytes 12292
  186.2 4.9 %copy-start.11 = (bf16[1,64,64]{2,1,0:T(8,128)(2,1)S(1)}, bf16[1,64,64]{2,1,0:T(8,128)(2,1)}, u32[]{:S(2)}) copy-start(bf16[1,64,64]{2,1,0:T(8,128)(2,1)} %param.24) | copy-start | bytes 24580
  186.2 5.1 %copy-start.8 = (bf16[1,64,192]{1,2,0:T(8,128)(2,1)S(1)}, bf16[1,64,192]{1,2,0:T(8,128)(2,1)}, u32[]{:S(2)}) copy-start(bf16[1,64,192]{1,2,0:T(8,128)(2,1)} %copy-done.7) | copy-start | bytes 73732
  186.2 5.3 %copy-start.2 = (bf16[16,64,64]{2,1,0:T(8,128)(2,1)S(1)}, bf16[16,64,64]{2,1,0:T(8,128)(2,1)}, u32[]{:S(2)}) copy-start(bf16[16,64,64]{2,1,0:T(8,128)(2,1)} %param.21) | copy-start | bytes 393220
  (1 other events, 4.6 us)
